TPU v7x, 32 devices: a whole 2x2x4 slice. The times are simulated.
32 devices in a mesh: var: 8 (over z, core), samp: 4 (over y, x).
Axes of the slice: x: 2, y: 2, z: 4, core: 2. Of those that a mesh axis runs over, the one named last changes fastest.
Arguments:
- geno: bfloat16 [8192, 16384], P('samp', 'var'), may hold values from -5 to 5
- scale_index: int32 [64, 16384], P('samp', 'var'), may hold values from 0 to 15
- scale_table: float32 [16], replicated, may hold values from 0.25 to 4
- residual: float32 [8, 8192], P(None, 'samp'), may hold values from -6 to 6
- beta_active: float32 [8, 3584], P(None, 'var'), may hold values from -6 to 6
- block_inverse: float32 [16, 256, 256], P('var'), may hold values from -1 to 4
- active_ids: int32 [3584], P('var'), may hold values from 0 to 16383, as said below
- admit_ids: int32 [512], P('var'), may hold values from 0 to 16383, as said below
Outputs:
- scores: float32 [8, 16384], P(None, 'var')
- coefficients: float32 [8, 4096], P(None, 'var')
- residual_out: float32 [8, 8192], P(None, 'samp')
Inputs may be any that keep to these rules, and one draw needn't show every extreme that they name: Variant ids, all different from one another and from those of admit_ids. The fitting slots of one index of var are its 448 entries of active_ids followed by its 64 entries of admit_ids; of these 512 slots at most 128 name variants held by any one index of var, and for every index of var some one holder reaches exactly 128. `admit_ids`: variant ids, as for active_ids.
All inputs are finite; a program needn't handle non-finite values.
Results may differ from a plain program's by a relative error of at most 0.004.
Values may be sent and summed in bfloat16 or wider, within the bound.
A program may use at most 128 MiB of HBM per device.

v0:
```python
import math
import jax
import jax.numpy as jnp
from jax import lax
from jax.sharding import PartitionSpec as P

PASSES = 3
penalty = 0.5
epsilon = 1e-06


def dequantize(values, indices, lookup):
    levels = lookup.shape[0]
    onehot = (indices[:, :, None] == jnp.arange(levels, dtype=jnp.int32)).astype(jnp.float32)
    scales = jnp.dot(onehot, lookup, precision=lax.Precision.HIGHEST)
    groups = indices.shape[0]
    widened = (
        values.reshape(groups, values.shape[0] // groups, values.shape[1]).astype(jnp.float32)
        * scales[:, None, :]
    )
    return widened.reshape(values.shape).astype(jnp.bfloat16)


def slot_layout(variant_ids, var_width, var_count):
    holder = variant_ids // var_width
    column = variant_ids % var_width
    owner_marks = (holder[..., None] == jnp.arange(var_count, dtype=jnp.int32)).astype(jnp.int32)
    before = jnp.cumsum(owner_marks, axis=-2) - owner_marks
    serial = jnp.sum(before * owner_marks, -1)
    return (holder, column, serial)


def block_update(gradient, coeffs, inverse):
    phenos, fit_width = gradient.shape
    blocks, block_size = (inverse.shape[0], inverse.shape[1])
    inner_term = (gradient - penalty * coeffs).reshape(phenos, blocks, block_size)
    direction = jnp.einsum("bij,pbj->pbi", inverse, inner_term, precision=lax.Precision.HIGHEST)
    return direction.reshape(phenos, fit_width).astype(jnp.bfloat16)


def on_device(
    geno, scale_index, scale_table, residual, beta_active, block_inverse, active_ids, admit_ids
):
    var_count = lax.axis_size("var")
    var_rank = lax.axis_index("var")
    samp_rows, var_width = geno.shape
    inv_root = 1.0 / math.sqrt(samp_rows * lax.axis_size("samp"))
    phenos = residual.shape[0]
    local_ids = jnp.concatenate([active_ids, admit_ids])
    fit_width = local_ids.shape[0]
    capacity = 2 * fit_width // var_count
    dequant = dequantize(geno, scale_index, scale_table)
    resid_low = residual.astype(jnp.bfloat16)
    screened = (
        lax.psum(jnp.dot(resid_low, dequant, preferred_element_type=jnp.float32), "samp") * inv_root
    )
    all_ids = lax.all_gather(local_ids, "var", axis=0, tiled=True).reshape(var_count, fit_width)
    holder, column, serial = slot_layout(all_ids, var_width, var_count)
    held_here = holder == var_rank
    wanted = held_here[:, None, :] & (
        serial[:, None, :] == jnp.arange(capacity, dtype=jnp.int32)[None, :, None]
    )
    source_column = jnp.sum(jnp.where(wanted, column[:, None, :], 0), -1).reshape(-1)
    present = jnp.any(wanted, -1).reshape(-1)
    selected = jnp.where(
        present[None, :], jnp.take(dequant, source_column, axis=1), jnp.zeros((), jnp.bfloat16)
    )
    position = lax.dynamic_index_in_dim(holder * capacity + serial, var_rank, 0, keepdims=False)
    coeffs = jnp.concatenate([beta_active, jnp.zeros((phenos, admit_ids.shape[0]), jnp.float32)], 1)
    current = residual
    for pass_index in range(PASSES):
        partial_sums = lax.psum(
            jnp.dot(resid_low, selected, preferred_element_type=jnp.float32), "samp"
        )
        routed = lax.all_to_all(partial_sums, "var", split_axis=1, concat_axis=1, tiled=True)
        gradient = jnp.take(routed, position, axis=1) * inv_root
        direction = block_update(gradient, coeffs, block_inverse)
        placed = (
            jnp.zeros((phenos, var_count * capacity), jnp.bfloat16).at[:, position].set(direction)
        )
        returned = lax.all_to_all(placed, "var", split_axis=1, concat_axis=1, tiled=True)
        partial_update = jnp.einsum(
            "pc,sc->ps", returned, selected, preferred_element_type=jnp.float32
        )
        update = lax.psum(partial_update, "var") * inv_root
        cross_sum, square = lax.psum(
            (jnp.sum(current * update, 1), jnp.sum(update * update, 1)), "samp"
        )
        factor = (cross_sum / (square + epsilon))[:, None]
        current = current - factor * update
        coeffs = coeffs + factor * direction.astype(jnp.float32)
        if pass_index + 1 < PASSES:
            resid_low = current.astype(jnp.bfloat16)
    return (screened, coeffs, current)


def solution(mesh):
    placed = (
        P("samp", "var"),
        P("samp", "var"),
        P(),
        P(None, "samp"),
        P(None, "var"),
        P("var", None, None),
        P("var"),
        P("var"),
    )
    return jax.shard_map(
        on_device,
        mesh=mesh,
        in_specs=placed,
        out_specs=(P(None, "var"), P(None, "var"), P(None, "samp")),
        check_vma=False,
    )
```

profile of v0, /device:TPU:0, one launch (start us, length us, event | category | flops | bytes accessed | tf_op | source)
XLA Modules:
  0.0 450.3 jit_solution(15364064158792349478)
XLA Ops:
  8.0 1.7 fusion.3
  9.7 0.3 copy.93
  10.1 12.3 %copy.78 = bf16[2048,2048]{0,1:T(8,128)(2,1)} copy(bf16[2048,2048]{1,0:T(8,128)(2,1)} %param.10) | data formatting | bytes 16777216 | tf_op args[0]
  22.5 14.5 %all-gather = s32[8,1,512]{2,1,0:T(1,128)S(1)} all-gather(s32[1,1,512]{2,1,0:T(1,128)S(1)} %bitcast.157), channel_id=1, replica_groups=mesh['var'=8,'samp'=4] {'var'}, dimensions={0}, use_global_device_ids=true | all-gather | bytes 18432 | tf_op jit(solution)/shard_map/all_gather | solution.py:57
  37.0 9.0 %reduce-window.6 = s32[8,8,4,128]{3,1,2,0:T(8,128)S(1)} reduce-window(s32[8,8,4,128]{3,1,2,0:T(8,128)S(1)} %fusion.13, s32[]{:T(128)} %constant.73.clone.1), window={size=1x1x1x128 pad=0_0x0_0x0_0x127_0}, to_apply=%region_1.2 | reduce-window | flops 4161536 | bytes 262148 | tf_op jit(solution)/shard_map/reduce-window
  46.1 0.3 copy.79
  46.6 0.1 fusion.6
  46.7 0.4 fusion.2
  47.1 0.5 select_reduce_fusion
  47.6 4.6 %mul.124 = f32[16,128,2048]{1,0,2:T(8,128)S(1)} broadcast(f32[16,2048]{0,1:T(8,128)S(1)} %bitcast.133), dimensions={0,2} | broadcast | bytes 16908288 | tf_op jit(solution)/shard_map/mul | solution.py:18
  52.2 9.2 %fusion = bf16[2048,2048]{0,1:T(8,128)(2,1)} fusion(f32[256,8,16,128]{3,2,1,0:T(8,128)S(1)} %bitcast.130, bf16[2048,2048]{0,1:T(8,128)(2,1)S(1)} %bitcast.132), kind=kLoop, calls=%fused_computation.8 | loop fusion | flops 12582912 | bytes 33554432 | tf_op jit(solution)/shard_map/convert_element_type | solution.py:21
  61.4 13.3 %gather_fusion = bf16[1024,2048]{1,0:T(8,128)(2,1)} fusion(bf16[2048,2048]{0,1:T(8,128)(2,1)} %fusion, s32[1024]{0:T(1024)S(1)} %broadcast_clamp_fusion), kind=kCustom, calls=%fused_computation.3 | custom fusion | bytes 8392704 | tf_op jit(solution)/shard_map/jit(_take)/gather | solution.py:66
  74.7 2.8 select_select_fusion
  77.5 2.0 copy-done.1
  79.5 1.2 convolution_bitcast_fusion.3
  80.6 16.9 %psum.92 = f32[8,8,128]{2,0,1:T(8,128)} all-reduce(f32[8,8,128]{2,0,1:T(8,128)S(1)} %convolution_bitcast_fusion.3), channel_id=1, replica_groups=mesh['var'=8,'samp'=4] {'samp'}, use_global_device_ids=true, to_apply=%region_6.7 | all-reduce | flops 8192 | bytes 65536 | tf_op jit(solution)/shard_map/psum | solution.py:72
  97.5 3.4 all-to-all-start
  100.9 0.2 all-reduce.11.cloned.1.call-start
  101.2 5.5 %all-to-all-done = f32[8,8,128]{2,0,1:T(8,128)S(1)} async-done(((f32[8,8,128]{2,0,1:T(8,128)}), f32[8,8,128]{2,0,1:T(8,128)S(1)}, u32[]{:S(2)}, u32[]{:S(2)}) %all-to-all-start) | async-done | bytes 32800 | tf_op jit(solution)/shard_map/all_to_all | solution.py:75
  106.6 0.2 copy.81
  106.8 1.0 gather_fusion.1
  108.0 0.5 convolution_convert_fusion.2
  108.5 0.2 copy.83
  108.7 1.8 scatter_custom_fusion
  110.7 8.0 %all_to_all.72 = bf16[8,8,128]{2,0,1:T(8,128)(2,1)S(1)} all-to-all(bf16[8,8,128]{2,0,1:T(8,128)(2,1)S(1)} %copy.84), channel_id=1, replica_groups=mesh['var'=8,'samp'=4] {'var'}, dimensions={1} | all-to-all | bytes 32768 | tf_op jit(solution)/shard_map/all_to_all | solution.py:81
  118.7 3.5 fusion.24
  122.2 51.3 %all-reduce.11.cloned.1.call-done = f32[8,2048]{1,0:T(8,128)} async-done(((f32[8,2048]{1,0:T(8,128)}), f32[8,2048]{1,0:T(8,128)}) %all-reduce.11.cloned.1.call-update) | async-done | bytes 65552 | tf_op jit(solution)/shard_map/psum | solution.py:85
  173.5 1.0 multiply_reduce_fusion.4
  174.5 9.8 %all-reduce.3 = (f32[8]{0:T(128)S(1)}, f32[8]{0:T(128)S(1)}) all-reduce(f32[8]{0:T(128)S(1)} %get-tuple-element.21, f32[8]{0:T(128)S(1)} %get-tuple-element.20), channel_id=1, replica_groups=mesh['var'=8,'samp'=4] {'samp'}, use_global_device_ids=true, to_apply=%region_10.12 | all-reduce | flops 16 | bytes 128 | tf_op jit(solution)/shard_map/psum | solution.py:86
  184.4 0.9 multiply_subtract_fusion.2
  185.3 3.4 convolution_bitcast_fusion.2
  188.7 14.4 %psum.96 = f32[8,8,128]{2,0,1:T(8,128)S(1)} all-reduce(f32[8,8,128]{2,0,1:T(8,128)S(1)} %convolution_bitcast_fusion.2), channel_id=1, replica_groups=mesh['var'=8,'samp'=4] {'samp'}, use_global_device_ids=true, to_apply=%region_13.15 | all-reduce | flops 8192 | bytes 65536 | tf_op jit(solution)/shard_map/psum | solution.py:72
  203.0 8.3 %all_to_all.73 = f32[8,8,128]{2,0,1:T(8,128)S(1)} all-to-all(f32[8,8,128]{2,0,1:T(8,128)S(1)} %psum.96), channel_id=1, replica_groups=mesh['var'=8,'samp'=4] {'var'}, dimensions={1} | all-to-all | bytes 65536 | tf_op jit(solution)/shard_map/all_to_all | solution.py:75
  211.3 0.2 copy.85
  211.5 1.0 gather_fusion.2
  212.8 0.5 convolution_convert_fusion.1
  213.3 0.2 copy.87
  213.5 1.8 scatter_custom_fusion.1
  215.4 8.0 %all_to_all.74 = bf16[8,8,128]{2,0,1:T(8,128)(2,1)S(1)} all-to-all(bf16[8,8,128]{2,0,1:T(8,128)(2,1)S(1)} %copy.88), channel_id=1, replica_groups=mesh['var'=8,'samp'=4] {'var'}, dimensions={1} | all-to-all | bytes 32768 | tf_op jit(solution)/shard_map/all_to_all | solution.py:81
  223.4 3.5 fusion.21
  226.9 52.2 %all-reduce.13.cloned.1.call-done = f32[8,2048]{1,0:T(8,128)} async-done(((f32[8,2048]{1,0:T(8,128)}), f32[8,2048]{1,0:T(8,128)}) %all-reduce.13.cloned.1.call-update) | async-done | bytes 65552 | tf_op jit(solution)/shard_map/psum | solution.py:85
  279.1 1.0 multiply_reduce_fusion.2
  280.1 9.8 %all-reduce.2 = (f32[8]{0:T(128)S(1)}, f32[8]{0:T(128)S(1)}) all-reduce(f32[8]{0:T(128)S(1)} %get-tuple-element.19, f32[8]{0:T(128)S(1)} %get-tuple-element.18), channel_id=1, replica_groups=mesh['var'=8,'samp'=4] {'samp'}, use_global_device_ids=true, to_apply=%region_17.19 | all-reduce | flops 16 | bytes 128 | tf_op jit(solution)/shard_map/psum | solution.py:86
  290.0 0.9 multiply_subtract_fusion.1
  290.9 3.4 convolution_bitcast_fusion.1
  294.3 14.4 %psum.100 = f32[8,8,128]{2,0,1:T(8,128)S(1)} all-reduce(f32[8,8,128]{2,0,1:T(8,128)S(1)} %convolution_bitcast_fusion.1), channel_id=1, replica_groups=mesh['var'=8,'samp'=4] {'samp'}, use_global_device_ids=true, to_apply=%region_20.22 | all-reduce | flops 8192 | bytes 65536 | tf_op jit(solution)/shard_map/psum | solution.py:72
  308.6 8.3 %all_to_all.75 = f32[8,8,128]{2,0,1:T(8,128)S(1)} all-to-all(f32[8,8,128]{2,0,1:T(8,128)S(1)} %psum.100), channel_id=1, replica_groups=mesh['var'=8,'samp'=4] {'var'}, dimensions={1} | all-to-all | bytes 65536 | tf_op jit(solution)/shard_map/all_to_all | solution.py:75
  316.9 0.2 copy.89
  317.1 1.0 gather_fusion.3
  318.3 0.5 convolution_convert_fusion
  318.9 0.2 copy.91
  319.1 1.8 scatter_custom_fusion.2
  320.9 0.7 copy.92
  321.6 3.3 all-to-all-start.5
  325.0 0.3 all-reduce.9.cloned.1.call-start
  325.2 6.3 %convolution_bitcast_fusion = f32[8,2048]{1,0:T(8,128)} fusion(bf16[2048,2048]{0,1:T(8,128)(2,1)} %fusion, f32[8,2048]{1,0:T(8,128)S(1)} %copy-done.2), kind=kOutput, calls=%fused_computation.10 | convolution fusion | flops 67125248 | bytes 8519680 | tf_op jit(solution)/shard_map/dot_general | solution.py:55
  331.6 3.5 fusion.18
  335.1 38.0 %all-reduce.9.cloned.1.call-done = f32[8,2048]{1,0:T(8,128)} async-done(((f32[8,2048]{1,0:T(8,128)}), f32[8,2048]{1,0:T(8,128)}) %all-reduce.9.cloned.1.call-update) | async-done | bytes 65552 | tf_op jit(solution)/shard_map/psum | solution.py:55
  373.1 1.5 broadcast_multiply_fusion
  374.6 55.2 %all-reduce.15.cloned.1.call-done = f32[8,2048]{1,0:T(8,128)} async-done(((f32[8,2048]{1,0:T(8,128)}), f32[8,2048]{1,0:T(8,128)}) %all-reduce.15.cloned.1.call-update) | async-done | bytes 65552 | tf_op jit(solution)/shard_map/psum | solution.py:85
  429.8 1.0 multiply_reduce_fusion
  430.8 9.8 %all-reduce.1 = (f32[8]{0:T(128)S(1)}, f32[8]{0:T(128)S(1)}) all-reduce(f32[8]{0:T(128)S(1)} %get-tuple-element.17, f32[8]{0:T(128)S(1)} %get-tuple-element.16), channel_id=1, replica_groups=mesh['var'=8,'samp'=4] {'samp'}, use_global_device_ids=true, to_apply=%region_24.26 | all-reduce | flops 16 | bytes 128 | tf_op jit(solution)/shard_map/psum | solution.py:86
  440.6 0.7 multiply_add_fusion
  441.3 1.5 multiply_subtract_fusion
  (50 shorter events, 1.3 us)
Async XLA Ops:
  8.0 100.0 %copy-start = (f32[2,256,256]{2,1,0:T(8,128)S(1)}, f32[2,256,256]{2,1,0:T(8,128)}, u32[]{:S(2)}) copy-start(f32[2,256,256]{2,1,0:T(8,128)} %param.15) | copy-start | bytes 1572868
  10.0 12.4 %copy-start.4 = (s32[448]{0:T(512)S(1)}, s32[448]{0:T(512)}, u32[]{:S(2)}) copy-start(s32[448]{0:T(512)} %param.16) | copy-start | bytes 5380
  10.0 12.3 %copy-start.5 = (s32[64]{0:T(128)S(1)}, s32[64]{0:T(128)}, u32[]{:S(2)}) copy-start(s32[64]{0:T(128)} %param.17) | copy-start | bytes 772
  46.5 5.7 %slice-start = ((s8[8388608]{0:T(1024)(128)(4,1)}), s8[4194304]{0:T(1024)(128)(4,1)S(1)}, s32[]{:S(2)}) async-start(s8[8388608]{0:T(1024)(128)(4,1)} %bitcast.131), calls=%async_computation.10 | async-start | bytes 8388608
  47.6 4.6 %slice-start.1 = ((s8[8388608]{0:T(1024)(128)(4,1)}), s8[4194304]{0:T(1024)(128)(4,1)S(1)}, s32[]{:S(2)}) async-start(s8[8388608]{0:T(1024)(128)(4,1)} %bitcast.131), calls=%async_computation.11 | async-start | bytes 8388608
  74.7 4.8 %copy-start.2 = (f32[8,2048]{1,0:T(8,128)S(1)}, f32[8,2048]{1,0:T(8,128)}, u32[]{:S(2)}) copy-start(f32[8,2048]{1,0:T(8,128)} %param.13) | copy-start | bytes 196612
  77.5 2.0 copy-start.1
  79.5 28.5 %copy-start.3 = (f32[8,448]{1,0:T(8,128)S(1)}, f32[8,448]{1,0:T(8,128)}, u32[]{:S(2)}) copy-start(f32[8,448]{1,0:T(8,128)} %param.14) | copy-start | bytes 43012
  97.5 9.1 %all-to-all-start = ((f32[8,8,128]{2,0,1:T(8,128)}), f32[8,8,128]{2,0,1:T(8,128)S(1)}, u32[]{:S(2)}, u32[]{:S(2)}) async-start(f32[8,8,128]{2,0,1:T(8,128)} %psum.92), calls=%async_computation | async-start | bytes 65536 | tf_op jit(solution)/shard_map/all_to_all | solution.py:75
  100.9 72.6 %all-reduce.11.cloned.1.call-start = ((), (), s32[]{:S(2)}) async-start(), calls=%async_computation.7 | async-start | bytes 131072 | tf_op jit(solution)/shard_map/psum | solution.py:85
  122.2 156.9 %all-reduce.13.cloned.1.call-start = ((), (), s32[]{:S(2)}) async-start(), calls=%async_computation.8 | async-start | bytes 131072 | tf_op jit(solution)/shard_map/psum | solution.py:85
  321.6 10.0 %all-to-all-start.5 = ((bf16[8,8,128]{2,0,1:T(8,128)(2,1)}), bf16[8,8,128]{2,0,1:T(8,128)(2,1)S(1)}, u32[]{:S(2)}, u32[]{:S(2)}) async-start(bf16[8,8,128]{2,0,1:T(8,128)(2,1)} %copy.92), calls=%async_computation.5 | async-start | bytes 32768 | tf_op jit(solution)/shard_map/all_to_all | solution.py:81
  325.0 48.1 %all-reduce.9.cloned.1.call-start = ((), (), s32[]{:S(2)}) async-start(), calls=%async_computation.6 | async-start | bytes 131072 | tf_op jit(solution)/shard_map/psum | solution.py:55
  331.5 98.2 %all-reduce.15.cloned.1.call-start = ((), (), s32[]{:S(2)}) async-start(), calls=%async_computation.9 | async-start | bytes 131072 | tf_op jit(solution)/shard_map/psum | solution.py:85
Sparse Core Ops, SparseCore 0:
  122.3 51.1 all-reduce.10
  227.1 52.0 all-reduce.12
Sparse Core Ops, SparseCore 1:
  331.6 41.4 all-reduce.8
  375.3 54.4 all-reduce.14
where the time goes:
time: 452 us; the launch traced here: 450 us
  waiting for transfers between devices  202 us (45%)
  blocking collectives  122 us (27%)
  local copies, waits for them, and re-layouts  43.8 us (10%)
  other arithmetic  31 us (7%)
  matrix products  27.8 us (6%)
  between operations  15.9 us (4%)
  starting transfers between devices  7.27 us (2%)
    psum x3, waiting for transfers between devices, on_device(): update = lax.psum(partial_update, 'var') * inv_root  159 us
    psum x3, blocking collectives, on_device(): lax.psum(jnp.dot(resid_low, selected, preferred_element_type=jnp.float32)...  45.6 us
    psum x1, waiting for transfers between devices, on_device(): lax.psum(jnp.dot(resid_low, dequant, preferred_element_type=jnp.float32),...  38 us
    psum x3, blocking collectives, on_device(): lax.psum((jnp.sum(current * update, 1), jnp.sum(update * update, 1)), 'sa...  29.5 us
    all_to_all x2, blocking collectives, on_device(): lax.all_to_all(partial_sums, 'var', split_axis=1, concat_axis=1, tiled=True)  16.6 us
    all_to_all x2, blocking collectives, on_device(): lax.all_to_all(placed, 'var', split_axis=1, concat_axis=1, tiled=True)  16 us
    all_gather x1, blocking collectives, on_device(): lax.all_gather(local_ids, 'var', axis=0, tiled=True)  14.5 us
    unnamed x17, local copies, waits for them, and re-layouts  14.3 us
  transfers between devices with their start and end apart: 6, of which 5 were waited for; matrix products, arithmetic and copies ran while one was open for 2% of the time, Pallas kernels for 0%

commit v1 on v0

--- a/solution.py
+++ b/solution.py
@@ -72,7 +72,15 @@
         partial_sums = lax.psum(
             jnp.dot(resid_low, selected, preferred_element_type=jnp.float32), "samp"
         )
-        routed = lax.all_to_all(partial_sums, "var", split_axis=1, concat_axis=1, tiled=True)
+        routed = jnp.concatenate(
+            lax.all_to_all(
+                jnp.stack(jnp.split(partial_sums, lax.axis_size("var"), axis=1), axis=0),
+                axis_name="var",
+                split_axis=0,
+                concat_axis=0,
+            ),
+            axis=1,
+        )
         gradient = jnp.take(routed, position, axis=1) * inv_root
         direction = block_update(gradient, coeffs, block_inverse)
         placed = (

time: 452 us -> 456 us (level)
  local copies, waits for them, and re-layouts: 43.8 us -> 48.6 us
    unnamed x17 -> x38, local copies, waits for them, and re-layouts: 14.3 us -> 18.5 us
where the time goes in v1:
time: 456 us; the launch traced here: 455 us
  waiting for transfers between devices  202 us (44%)
  blocking collectives  122 us (27%)
  local copies, waits for them, and re-layouts  48.6 us (11%)
  other arithmetic  31 us (7%)
  matrix products  27.8 us (6%)
  between operations  16 us (4%)
  starting transfers between devices  7.27 us (2%)
    psum x3, waiting for transfers between devices, on_device(): update = lax.psum(partial_update, 'var') * inv_root  159 us
    psum x3, blocking collectives, on_device(): lax.psum(jnp.dot(resid_low, selected, preferred_element_type=jnp.float32)...  45 us
    psum x1, waiting for transfers between devices, on_device(): lax.psum(jnp.dot(resid_low, dequant, preferred_element_type=jnp.float32),...  38 us
    psum x3, blocking collectives, on_device(): lax.psum((jnp.sum(current * update, 1), jnp.sum(update * update, 1)), 'sa...  29.5 us
    unnamed x38, local copies, waits for them, and re-layouts  18.5 us
    all_to_all x2, blocking collectives, on_device(): lax.all_to_all(jnp.stack(jnp.split(partial_sums, lax.axis_size('var'), ax...  16.6 us
    all_to_all x2, blocking collectives, on_device(): lax.all_to_all(placed, 'var', split_axis=1, concat_axis=1, tiled=True)  16 us
    all_gather x1, blocking collectives, on_device(): lax.all_gather(local_ids, 'var', axis=0, tiled=True)  14.5 us
  transfers between devices with their start and end apart: 6, of which 5 were waited for; matrix products, arithmetic and copies ran while one was open for 2% of the time, Pallas kernels for 0%

profile of v1, /device:TPU:0, one launch (start us, length us, event | category | flops | bytes accessed | tf_op | source)
XLA Modules:
  0.0 454.7 jit_solution(18445301802834207062)
XLA Ops:
  8.0 1.7 fusion.3
  9.7 0.3 copy.90
  10.1 12.3 %copy.75 = bf16[2048,2048]{0,1:T(8,128)(2,1)} copy(bf16[2048,2048]{1,0:T(8,128)(2,1)} %param.10) | data formatting | bytes 16777216 | tf_op args[0]
  22.5 14.5 %all-gather = s32[8,1,512]{2,1,0:T(1,128)S(1)} all-gather(s32[1,1,512]{2,1,0:T(1,128)S(1)} %bitcast.253), channel_id=1, replica_groups=mesh['var'=8,'samp'=4] {'var'}, dimensions={0}, use_global_device_ids=true | all-gather | bytes 18432 | tf_op jit(solution)/shard_map/all_gather | solution.py:57
  37.0 9.0 %reduce-window.6 = s32[8,8,4,128]{3,1,2,0:T(8,128)S(1)} reduce-window(s32[8,8,4,128]{3,1,2,0:T(8,128)S(1)} %fusion.13, s32[]{:T(128)} %constant.73.clone.1), window={size=1x1x1x128 pad=0_0x0_0x0_0x127_0}, to_apply=%region_1.2 | reduce-window | flops 4161536 | bytes 262148 | tf_op jit(solution)/shard_map/reduce-window
  46.1 0.3 copy.76
  46.7 0.4 fusion.2
  47.1 0.5 select_reduce_fusion
  47.6 4.6 %mul.124 = f32[16,128,2048]{1,0,2:T(8,128)S(1)} broadcast(f32[16,2048]{0,1:T(8,128)S(1)} %bitcast.229), dimensions={0,2} | broadcast | bytes 16908288 | tf_op jit(solution)/shard_map/mul | solution.py:18
  52.2 9.2 %fusion = bf16[2048,2048]{0,1:T(8,128)(2,1)} fusion(f32[256,8,16,128]{3,2,1,0:T(8,128)S(1)} %bitcast.226, bf16[2048,2048]{0,1:T(8,128)(2,1)S(1)} %bitcast.228), kind=kLoop, calls=%fused_computation.8 | loop fusion | flops 12582912 | bytes 33554432 | tf_op jit(solution)/shard_map/convert_element_type | solution.py:21
  61.4 13.3 %gather_fusion = bf16[1024,2048]{1,0:T(8,128)(2,1)} fusion(bf16[2048,2048]{0,1:T(8,128)(2,1)} %fusion, s32[1024]{0:T(1024)S(1)} %broadcast_clamp_fusion), kind=kCustom, calls=%fused_computation.3 | custom fusion | bytes 8392704 | tf_op jit(solution)/shard_map/jit(_take)/gather | solution.py:66
  74.7 2.8 select_select_fusion
  77.5 2.0 copy-done.1
  79.5 1.2 convolution_bitcast_fusion.1
  80.6 16.3 %psum.92 = f32[8,1024]{1,0:T(8,128)S(1)} all-reduce(f32[8,1024]{1,0:T(8,128)S(1)} %convolution_bitcast_fusion.1), channel_id=1, replica_groups=mesh['var'=8,'samp'=4] {'samp'}, use_global_device_ids=true, to_apply=%region_6.7 | all-reduce | flops 8192 | bytes 65536 | tf_op jit(solution)/shard_map/psum | solution.py:72
  96.9 0.6 constant_dynamic-update-slice_fusion.7
  97.5 0.6 constant_dynamic-update-slice_fusion.6
  98.1 0.6 constant_dynamic-update-slice_fusion.5
  98.7 0.6 constant_dynamic-update-slice_fusion.4
  99.3 0.6 constant_dynamic-update-slice_fusion.3
  99.9 0.6 constant_dynamic-update-slice_fusion.2
  100.5 0.6 constant_dynamic-update-slice_fusion.1
  101.1 0.6 constant_dynamic-update-slice_fusion
  101.7 3.4 all-to-all-start
  105.4 5.5 %all-to-all-done = f32[8,8,128]{2,1,0:T(8,128)S(1)} async-done(((f32[8,8,128]{2,1,0:T(8,128)}), f32[8,8,128]{2,1,0:T(8,128)S(1)}, u32[]{:S(2)}, u32[]{:S(2)}) %all-to-all-start) | async-done | bytes 32800 | tf_op jit(solution)/shard_map/all_to_all | solution.py:76
  111.0 1.0 gather_fusion.1
  112.2 0.5 convolution_convert_fusion.2
  112.9 1.8 scatter_custom_fusion
  114.8 8.0 %all_to_all.51 = bf16[8,8,128]{2,0,1:T(8,128)(2,1)S(1)} all-to-all(bf16[8,8,128]{2,0,1:T(8,128)(2,1)S(1)} %copy.81), channel_id=1, replica_groups=mesh['var'=8,'samp'=4] {'var'}, dimensions={1} | all-to-all | bytes 32768 | tf_op jit(solution)/shard_map/all_to_all | solution.py:89
  122.9 3.5 fusion.26
  126.4 51.3 %all-reduce.11.cloned.1.call-done = f32[8,2048]{1,0:T(8,128)} async-done(((f32[8,2048]{1,0:T(8,128)}), f32[8,2048]{1,0:T(8,128)}) %all-reduce.11.cloned.1.call-update) | async-done | bytes 65552 | tf_op jit(solution)/shard_map/psum | solution.py:93
  177.7 1.0 multiply_reduce_fusion.4
  178.7 9.8 %all-reduce.3 = (f32[8]{0:T(128)S(1)}, f32[8]{0:T(128)S(1)}) all-reduce(f32[8]{0:T(128)S(1)} %get-tuple-element.21, f32[8]{0:T(128)S(1)} %get-tuple-element.20), channel_id=1, replica_groups=mesh['var'=8,'samp'=4] {'samp'}, use_global_device_ids=true, to_apply=%region_10.12 | all-reduce | flops 16 | bytes 128 | tf_op jit(solution)/shard_map/psum | solution.py:94
  188.5 0.9 multiply_subtract_fusion.2
  189.5 3.4 fusion.16
  192.8 14.4 %psum.96 = f32[8,1024]{1,0:T(8,128)S(1)} all-reduce(f32[8,1024]{1,0:T(8,128)S(1)} %fusion.16), channel_id=1, replica_groups=mesh['var'=8,'samp'=4] {'samp'}, use_global_device_ids=true, to_apply=%region_13.15 | all-reduce | flops 8192 | bytes 65536 | tf_op jit(solution)/shard_map/psum | solution.py:72
  207.3 8.3 %all_to_all.52 = f32[8,8,128]{2,1,0:T(8,128)S(1)} all-to-all(f32[8,8,128]{2,1,0:T(8,128)S(1)} %constant_dynamic-update-slice_fusion.8), channel_id=1, replica_groups=mesh['var'=8,'samp'=4] {'var'}, dimensions={0} | all-to-all | bytes 65536 | tf_op jit(solution)/shard_map/all_to_all | solution.py:76
  215.8 1.0 gather_fusion.2
  217.0 0.5 convolution_convert_fusion.1
  217.7 1.8 scatter_custom_fusion.1
  219.7 8.0 %all_to_all.53 = bf16[8,8,128]{2,0,1:T(8,128)(2,1)S(1)} all-to-all(bf16[8,8,128]{2,0,1:T(8,128)(2,1)S(1)} %copy.85), channel_id=1, replica_groups=mesh['var'=8,'samp'=4] {'var'}, dimensions={1} | all-to-all | bytes 32768 | tf_op jit(solution)/shard_map/all_to_all | solution.py:89
  227.7 3.5 fusion.23
  231.2 52.2 %all-reduce.13.cloned.1.call-done = f32[8,2048]{1,0:T(8,128)} async-done(((f32[8,2048]{1,0:T(8,128)}), f32[8,2048]{1,0:T(8,128)}) %all-reduce.13.cloned.1.call-update) | async-done | bytes 65552 | tf_op jit(solution)/shard_map/psum | solution.py:93
  283.4 1.0 multiply_reduce_fusion.2
  284.4 9.8 %all-reduce.2 = (f32[8]{0:T(128)S(1)}, f32[8]{0:T(128)S(1)}) all-reduce(f32[8]{0:T(128)S(1)} %get-tuple-element.19, f32[8]{0:T(128)S(1)} %get-tuple-element.18), channel_id=1, replica_groups=mesh['var'=8,'samp'=4] {'samp'}, use_global_device_ids=true, to_apply=%region_17.19 | all-reduce | flops 16 | bytes 128 | tf_op jit(solution)/shard_map/psum | solution.py:94
  294.2 0.9 multiply_subtract_fusion.1
  295.1 3.4 fusion.14
  298.5 14.4 %psum.100 = f32[8,1024]{1,0:T(8,128)S(1)} all-reduce(f32[8,1024]{1,0:T(8,128)S(1)} %fusion.14), channel_id=1, replica_groups=mesh['var'=8,'samp'=4] {'samp'}, use_global_device_ids=true, to_apply=%region_20.22 | all-reduce | flops 8192 | bytes 65536 | tf_op jit(solution)/shard_map/psum | solution.py:72
  313.0 8.3 %all_to_all.54 = f32[8,8,128]{2,1,0:T(8,128)S(1)} all-to-all(f32[8,8,128]{2,1,0:T(8,128)S(1)} %constant_dynamic-update-slice_fusion.16), channel_id=1, replica_groups=mesh['var'=8,'samp'=4] {'var'}, dimensions={0} | all-to-all | bytes 65536 | tf_op jit(solution)/shard_map/all_to_all | solution.py:76
  321.5 1.0 gather_fusion.3
  322.7 0.5 convolution_convert_fusion
  323.4 1.8 scatter_custom_fusion.2
  325.2 0.7 copy.89
  326.0 3.3 all-to-all-start.5
  329.3 0.3 all-reduce.9.cloned.1.call-start
  329.6 6.3 %convolution_bitcast_fusion = f32[8,2048]{1,0:T(8,128)} fusion(bf16[2048,2048]{0,1:T(8,128)(2,1)} %fusion, f32[8,2048]{1,0:T(8,128)S(1)} %copy-done.2), kind=kOutput, calls=%fused_computation.10 | convolution fusion | flops 67125248 | bytes 8519680 | tf_op jit(solution)/shard_map/dot_general | solution.py:55
  335.9 3.5 fusion.20
  339.4 38.0 %all-reduce.9.cloned.1.call-done = f32[8,2048]{1,0:T(8,128)} async-done(((f32[8,2048]{1,0:T(8,128)}), f32[8,2048]{1,0:T(8,128)}) %all-reduce.9.cloned.1.call-update) | async-done | bytes 65552 | tf_op jit(solution)/shard_map/psum | solution.py:55
  377.5 1.5 broadcast_multiply_fusion
  378.9 55.2 %all-reduce.15.cloned.1.call-done = f32[8,2048]{1,0:T(8,128)} async-done(((f32[8,2048]{1,0:T(8,128)}), f32[8,2048]{1,0:T(8,128)}) %all-reduce.15.cloned.1.call-update) | async-done | bytes 65552 | tf_op jit(solution)/shard_map/psum | solution.py:93
  434.2 1.0 multiply_reduce_fusion
  435.2 9.8 %all-reduce.1 = (f32[8]{0:T(128)S(1)}, f32[8]{0:T(128)S(1)}) all-reduce(f32[8]{0:T(128)S(1)} %get-tuple-element.17, f32[8]{0:T(128)S(1)} %get-tuple-element.16), channel_id=1, replica_groups=mesh['var'=8,'samp'=4] {'samp'}, use_global_device_ids=true, to_apply=%region_24.26 | all-reduce | flops 16 | bytes 128 | tf_op jit(solution)/shard_map/psum | solution.py:94
  445.0 0.7 multiply_add_fusion
  445.7 1.5 multiply_subtract_fusion
  (74 shorter events, 2.8 us)
Async XLA Ops:
  8.0 104.2 %copy-start = (f32[2,256,256]{2,1,0:T(8,128)S(1)}, f32[2,256,256]{2,1,0:T(8,128)}, u32[]{:S(2)}) copy-start(f32[2,256,256]{2,1,0:T(8,128)} %param.15) | copy-start | bytes 1572868
  10.0 12.4 %copy-start.4 = (s32[448]{0:T(512)S(1)}, s32[448]{0:T(512)}, u32[]{:S(2)}) copy-start(s32[448]{0:T(512)} %param.16) | copy-start | bytes 5380
  10.0 12.3 %copy-start.5 = (s32[64]{0:T(128)S(1)}, s32[64]{0:T(128)}, u32[]{:S(2)}) copy-start(s32[64]{0:T(128)} %param.17) | copy-start | bytes 772
  46.5 5.7 %slice-start = ((s8[8388608]{0:T(1024)(128)(4,1)}), s8[4194304]{0:T(1024)(128)(4,1)S(1)}, s32[]{:S(2)}) async-start(s8[8388608]{0:T(1024)(128)(4,1)} %bitcast.227), calls=%async_computation.10 | async-start | bytes 8388608
  47.6 4.6 %slice-start.1 = ((s8[8388608]{0:T(1024)(128)(4,1)}), s8[4194304]{0:T(1024)(128)(4,1)S(1)}, s32[]{:S(2)}) async-start(s8[8388608]{0:T(1024)(128)(4,1)} %bitcast.227), calls=%async_computation.11 | async-start | bytes 8388608
  74.7 4.8 %copy-start.2 = (f32[8,2048]{1,0:T(8,128)S(1)}, f32[8,2048]{1,0:T(8,128)}, u32[]{:S(2)}) copy-start(f32[8,2048]{1,0:T(8,128)} %param.13) | copy-start | bytes 196612
  77.5 2.0 copy-start.1
  79.5 32.7 %copy-start.3 = (f32[8,448]{1,0:T(8,128)S(1)}, f32[8,448]{1,0:T(8,128)}, u32[]{:S(2)}) copy-start(f32[8,448]{1,0:T(8,128)} %param.14) | copy-start | bytes 43012
  101.7 9.1 %all-to-all-start = ((f32[8,8,128]{2,1,0:T(8,128)}), f32[8,8,128]{2,1,0:T(8,128)S(1)}, u32[]{:S(2)}, u32[]{:S(2)}) async-start(f32[8,8,128]{2,1,0:T(8,128)} %constant_dynamic-update-slice_fusion), calls=%async_computation | async-start | bytes 65536 | tf_op jit(solution)/shard_map/all_to_all | solution.py:76
  105.1 72.6 %all-reduce.11.cloned.1.call-start = ((), (), s32[]{:S(2)}) async-start(), calls=%async_computation.7 | async-start | bytes 131072 | tf_op jit(solution)/shard_map/psum | solution.py:93
  126.4 157.0 %all-reduce.13.cloned.1.call-start = ((), (), s32[]{:S(2)}) async-start(), calls=%async_computation.8 | async-start | bytes 131072 | tf_op jit(solution)/shard_map/psum | solution.py:93
  326.0 10.0 %all-to-all-start.5 = ((bf16[8,8,128]{2,0,1:T(8,128)(2,1)}), bf16[8,8,128]{2,0,1:T(8,128)(2,1)S(1)}, u32[]{:S(2)}, u32[]{:S(2)}) async-start(bf16[8,8,128]{2,0,1:T(8,128)(2,1)} %copy.89), calls=%async_computation.5 | async-start | bytes 32768 | tf_op jit(solution)/shard_map/all_to_all | solution.py:89
  329.3 48.2 %all-reduce.9.cloned.1.call-start = ((), (), s32[]{:S(2)}) async-start(), calls=%async_computation.6 | async-start | bytes 131072 | tf_op jit(solution)/shard_map/psum | solution.py:55
  335.9 98.3 %all-reduce.15.cloned.1.call-start = ((), (), s32[]{:S(2)}) async-start(), calls=%async_computation.9 | async-start | bytes 131072 | tf_op jit(solution)/shard_map/psum | solution.py:93
Sparse Core Ops, SparseCore 0:
  126.5 51.1 all-reduce.10
  231.3 52.0 all-reduce.12
Sparse Core Ops, SparseCore 1:
  336.0 41.4 all-reduce.8
  379.6 54.4 all-reduce.14
